TPU v7x, 32 devices: a whole 2x2x4 slice. The times are simulated.
32 devices in a mesh: dp: 2 (over x), context: 4 (over z), tensor: 4 (over y, core).
Axes of the slice: x: 2, y: 2, z: 4, core: 2. Of those that a mesh axis runs over, the one named last changes fastest.
Arguments:
- queries: bfloat16 [2, 1024, 8192], P('dp', 'context', 'tensor'), may hold values from -45 to 45
- keys: bfloat16 [2, 1024, 1024], P('dp', 'context'), may hold values from -20 to 20
- values: bfloat16 [2, 1024, 1024], P('dp', 'context'), may hold values from -6 to 6
- out_weight: bfloat16 [8192, 8192], P('tensor'), may hold values from -0.0625 to 0.0625
- segment_ids: int32 [2, 1024], P('dp'), may hold values from 0 to 7, as said below
- loss_mask: int32 [2, 1024], P('dp', 'context'), may hold values from 0 to 1, as said below
- span_order: int32 [8], replicated, may hold values from 0 to 7, as said below
Outputs:
- weighted_out: bfloat16 [2, 1024, 8192], P('dp', 'context', 'tensor')
Inputs may be any that keep to these rules, and one draw needn't show every extreme that they name: `span_order`: a permutation of 0 .. 7. `segment_ids`: taken in order of sequence position pos (see the steps), a sequence's document numbers never fall; each sequence holds 8 documents. `loss_mask`: the first row of every sequence is 1.
All inputs are finite; a program needn't handle non-finite values.
Results may differ from a plain program's by a relative error of at most 0.018.
Values may be sent and summed in bfloat16 or wider, within the bound.
A program may use at most 128 MiB of HBM per device.

v0:
```python
import jax
import jax.numpy as jnp
from jax import lax
from jax.sharding import PartitionSpec as P

QH = 64
KVH = 8
HD = 128


def passed_along(value, axis, steps):
    count = lax.axis_size(axis)
    pairs = [(source, (source + steps) % count) for source in range(count)]
    return lax.ppermute(value, axis, pairs)


def per_device(queries, keys, values, out_weight, segment_ids, loss_mask, span_order):
    n_context = lax.axis_size("context")
    tok_rows = queries.shape[1]
    span_rows = tok_rows // 2
    heads_dev = queries.shape[2] // HD
    group = QH // KVH
    kv_dev = max(1, heads_dev // group)
    per_kv = heads_dev // kv_dev
    tensor_index = lax.axis_index("tensor")
    context_index = lax.axis_index("context")
    kv_first = tensor_index * heads_dev // group * HD
    key_local = lax.dynamic_slice_in_dim(keys[0], kv_first, kv_dev * HD, 1)
    value_local = lax.dynamic_slice_in_dim(values[0], kv_first, kv_dev * HD, 1)
    query_heads = queries[0].reshape(tok_rows, kv_dev, per_kv, HD)
    seg_all = segment_ids[0]
    n_spans = span_order.shape[0]
    factor = HD ** (-0.5)

    def positions(rows):
        span = rows // span_rows
        table = jnp.sum(
            jnp.where(
                span[:, None] == jnp.arange(n_spans, dtype=jnp.int32)[None, :],
                span_order[None, :],
                0,
            ),
            axis=1,
        )
        return table * span_rows + rows % span_rows

    query_first = context_index * tok_rows
    query_pos = positions(query_first + jnp.arange(tok_rows, dtype=jnp.int32))
    query_seg = lax.dynamic_slice_in_dim(seg_all, query_first, tok_rows)

    def attend(state, key_block, value_block, first_row):
        count_rows = key_block.shape[0]
        first_row = jnp.asarray(first_row, jnp.int32)
        key_pos = positions(first_row + jnp.arange(count_rows, dtype=jnp.int32))
        key_seg = lax.dynamic_slice_in_dim(seg_all, first_row, count_rows)
        allowed = (query_seg[:, None] == key_seg[None, :]) & (
            query_pos[:, None] >= key_pos[None, :]
        )
        best, total, accum = state
        key_heads = key_block.reshape(count_rows, kv_dev, HD)
        value_heads = value_block.reshape(count_rows, kv_dev, HD)
        scores = (
            jnp.einsum("qghd,kgd->ghqk", query_heads, key_heads, preferred_element_type=jnp.float32)
            * factor
        )
        scores = jnp.where(allowed, scores, -1e30)
        new_best = jnp.maximum(best, jnp.max(scores, axis=-1))
        correct = jnp.exp(best - new_best)
        probs = jnp.where(allowed, jnp.exp(scores - new_best[..., None]), 0.0)
        total = total * correct + jnp.sum(probs, axis=-1)
        update = jnp.einsum(
            "ghqk,kgd->ghqd",
            probs.astype(jnp.bfloat16),
            value_heads,
            preferred_element_type=jnp.float32,
        )
        accum = accum * correct[..., None] + update
        return (new_best, total, accum)

    initial = (
        jnp.full((kv_dev, per_kv, tok_rows), -1e30, jnp.float32),
        jnp.zeros((kv_dev, per_kv, tok_rows), jnp.float32),
        jnp.zeros((kv_dev, per_kv, tok_rows, HD), jnp.float32),
    )
    state = attend(initial, key_local, value_local, query_first)

    def turn(turn_index, carry):
        key_block, value_block, inner = carry
        key_block, value_block = passed_along((key_block, value_block), "context", 1)
        source = (context_index - turn_index) % n_context
        inner = attend(inner, key_block, value_block, source * tok_rows)
        return (key_block, value_block, inner)

    moved_keys, moved_values, state = lax.fori_loop(
        1, n_context, turn, (key_local, value_local, state)
    )
    best, total, accum = state
    heads_out = (accum / total[..., None]).astype(jnp.bfloat16)
    heads_out = jnp.transpose(heads_out, (2, 0, 1, 3)).reshape(tok_rows, heads_dev * HD)
    partial_value = jnp.dot(heads_out, out_weight, preferred_element_type=jnp.float32)
    summed = lax.psum_scatter(
        partial_value.astype(jnp.bfloat16), "tensor", scatter_dimension=1, tiled=True
    ).astype(jnp.float32)
    mask_rows = loss_mask[0].astype(jnp.float32)
    counted = lax.psum(jnp.sum(mask_rows), ("dp", "context"))
    scale_all = lax.axis_size("dp") * n_context * tok_rows
    weighted = (summed * (mask_rows * scale_all / counted)[:, None]).astype(jnp.bfloat16)
    return weighted[None]


def solution(mesh):
    in_specs = (
        P("dp", "context", "tensor"),
        P("dp", "context", None),
        P("dp", "context", None),
        P("tensor", None),
        P("dp", None),
        P("dp", "context"),
        P(),
    )
    out_specs = P("dp", "context", "tensor")
    return jax.shard_map(
        per_device, mesh=mesh, in_specs=in_specs, out_specs=out_specs, check_vma=False
    )
```

profile of v0, /device:TPU:0, one launch (start us, length us, event | category | flops | bytes accessed | tf_op | source)
XLA Modules:
  0.0 132.4 jit_solution(11098883301722410251)
XLA Ops:
  6.6 1.0 constant_dynamic-slice_fusion.1
  7.6 0.8 copy.49
  8.3 0.7 select_reduce_fusion.1
  9.1 1.5 %copy.27 = bf16[1,256,2048]{1,2,0:T(8,128)(2,1)S(1)} copy(bf16[1,256,2048]{2,1,0:T(8,128)(2,1)} %param.9) | data formatting | bytes 2097152 | tf_op args[0]
  10.5 0.7 copy.32
  11.4 1.8 %fusion.17 = (f32[2,8,256]{2,1,0:T(8,128)S(1)}, f32[2,256,256,8]{2,1,3,0:T(8,128)S(1)}) fusion(pred[256,256]{0,1:T(8,128)(4,1)S(1)} %compare_and_fusion.1, bf16[256,2,128,1]{0,2,3,1:T(8,128)(2,1)} %bitcast.26, bf16[256,2,8,128]{0,3,2,1:T(8,128)(2,1)S(1)} %bitcast.83), kind=kOutput, calls=%fused_computation.32 | convolution fusion | flops 271577088 | bytes 5455872 | tf_op jit(solution)/shard_map/qghd,kgd->ghqk/dot_general | solution.py:63
  13.2 1.9 %copy-done = f32[2,256,256,8]{2,1,3,0:T(8,128)} copy-done((f32[2,256,256,8]{2,1,3,0:T(8,128)}, f32[2,256,256,8]{2,1,3,0:T(8,128)S(1)}, u32[]{:S(2)}) %copy-start) | copy-done | bytes 4194328
  15.1 1.0 fusion.19
  16.1 0.7 copy.50
  16.9 3.4 %fusion.27 = f32[2,8,256,128]{3,2,1,0:T(8,128)S(1)} fusion(bf16[256,2,128,1]{0,2,3,1:T(8,128)(2,1)} %bitcast.28, f32[2,256,256,8]{2,1,3,0:T(8,128)} %copy-done, f32[2,8,256]{2,1,0:T(8,128)S(1)} %broadcast_maximum_fusion, pred[256,256]{0,1:T(8,128)(4,1)S(1)} %compare_and_fusion.1, f32[2,8,256]{2,1,0:T(8,128)S(1)} %get-tuple-element.388), kind=kOutput, calls=%fused_computation.43 | convolution fusion | flops 274202624 | bytes 6520832 | tf_op jit(solution)/shard_map/ghqk,kgd->ghqd/dot_general | solution.py:71
  20.3 40.2 %while.24 = (s32[]{:T(128)}, bf16[256,256]{0,1:T(8,128)(2,1)}, bf16[256,256]{0,1:T(8,128)(2,1)}, f32[2,8,256]{2,1,0:T(8,128)S(1)}, f32[2,8,256]{2,1,0:T(8,128)S(...) while((s32[]{:T(128)}, bf16[256,256]{0,1:T(8,128)(2,1)}, ...), condition=%wide.region_7.8_spmd, body=%wide.region_3.7_spmd.sunk | while | flops 551769344 | bytes 20196808 | solution.py:94
  20.3 3.1 %collective-permute-start = (bf16[256,256]{0,1:T(8,128)(2,1)}, bf16[256,256]{0,1:T(8,128)(2,1)S(1)}, u32[]{:S(2)}, u32[]{:S(2)}) collective-permute-start(bf16[256,256]{0,1:T(8,128)(2,1)} %get-tuple-element.494), channel_id=1, source_target_pairs={{0,4},{4,8},{8,12},{12,0},{1,5},{5,9},{9,13},{13,1},{2,6},{6,10},{... | collective-permute-start | bytes 393224 | tf_op jit(solution)/shard_map/while/body/eval_jaxpr/ppermute | solution.py:14
  23.4 1.6 %collective-permute-start.1 = (bf16[256,256]{0,1:T(8,128)(2,1)}, bf16[256,256]{0,1:T(8,128)(2,1)S(1)}, u32[]{:S(2)}, u32[]{:S(2)}) collective-permute-start(bf16[256,256]{0,1:T(8,128)(2,1)} %get-tuple-element.495), channel_id=1, source_target_pairs={{0,4},{4,8},{8,12},{12,0},{1,5},{5,9},{9,13},{13,1},{2,6},{6,10},{... | collective-permute-start | bytes 393224 | tf_op jit(solution)/shard_map/while/body/eval_jaxpr/ppermute | solution.py:14
  25.3 4.7 %collective-permute-done = bf16[256,256]{0,1:T(8,128)(2,1)S(1)} collective-permute-done((bf16[256,256]{0,1:T(8,128)(2,1)}, bf16[256,256]{0,1:T(8,128)(2,1)S(1)}, u32[]{:S(2)}, u32[]{:S(2)}) %collective-permute-start) | collective-permute-done | bytes 131104 | tf_op jit(solution)/shard_map/while/body/eval_jaxpr/ppermute | solution.py:14
  30.0 0.9 fusion.57
  30.9 1.0 fusion.58
  31.9 1.9 %multiply_add_fusion.5 = f32[2,8,256,128]{3,2,1,0:T(8,128)S(1)} fusion(f32[2,8,256,128]{3,2,1,0:T(8,128)S(1)} %get-tuple-element.498, bf16[256,2,128,1]{0,2,3,1:T(8,128)(2,1)S(1)} %bitcast.85, f32[2,256,256,8]{2,1,3,0:T(8,128)S(1)} %get-tuple-element.472, f32[2,8,256]{2,1,0:T(8,128)S(1)} %max.12, pred[256,256]{0,1:T(8,128)(4,1)S(1)} %compare_and_fusion.3, ...), kind=kOutput, calls=%fused_computation.6.clone.1 | convolution fusion | flops 274726912 | bytes 8617984 | tf_op jit(solution)/shard_map/while/body/eval_jaxpr/ghqk,kgd->ghqd/dot_general | solution.py:71
  35.1 1.6 %collective-permute-start.1 = (bf16[256,256]{0,1:T(8,128)(2,1)}, bf16[256,256]{0,1:T(8,128)(2,1)S(1)}, u32[]{:S(2)}, u32[]{:S(2)}) collective-permute-start(bf16[256,256]{0,1:T(8,128)(2,1)} %get-tuple-element.495), channel_id=1, source_target_pairs={{0,4},{4,8},{8,12},{12,0},{1,5},{5,9},{9,13},{13,1},{2,6},{6,10},{... | collective-permute-start | bytes 393224 | tf_op jit(solution)/shard_map/while/body/eval_jaxpr/ppermute | solution.py:14
  37.0 6.2 %collective-permute-done = bf16[256,256]{0,1:T(8,128)(2,1)S(1)} collective-permute-done((bf16[256,256]{0,1:T(8,128)(2,1)}, bf16[256,256]{0,1:T(8,128)(2,1)S(1)}, u32[]{:S(2)}, u32[]{:S(2)}) %collective-permute-start) | collective-permute-done | bytes 131104 | tf_op jit(solution)/shard_map/while/body/eval_jaxpr/ppermute | solution.py:14
  43.2 0.9 fusion.57
  44.1 1.0 fusion.58
  45.1 1.9 %multiply_add_fusion.5 = f32[2,8,256,128]{3,2,1,0:T(8,128)S(1)} fusion(f32[2,8,256,128]{3,2,1,0:T(8,128)S(1)} %get-tuple-element.498, bf16[256,2,128,1]{0,2,3,1:T(8,128)(2,1)S(1)} %bitcast.85, f32[2,256,256,8]{2,1,3,0:T(8,128)S(1)} %get-tuple-element.472, f32[2,8,256]{2,1,0:T(8,128)S(1)} %max.12, pred[256,256]{0,1:T(8,128)(4,1)S(1)} %compare_and_fusion.3, ...), kind=kOutput, calls=%fused_computation.6.clone.1 | convolution fusion | flops 274726912 | bytes 8617984 | tf_op jit(solution)/shard_map/while/body/eval_jaxpr/ghqk,kgd->ghqd/dot_general | solution.py:71
  48.7 6.6 %collective-permute-done = bf16[256,256]{0,1:T(8,128)(2,1)S(1)} collective-permute-done((bf16[256,256]{0,1:T(8,128)(2,1)}, bf16[256,256]{0,1:T(8,128)(2,1)S(1)}, u32[]{:S(2)}, u32[]{:S(2)}) %collective-permute-start) | collective-permute-done | bytes 131104 | tf_op jit(solution)/shard_map/while/body/eval_jaxpr/ppermute | solution.py:14
  55.3 0.9 fusion.57
  56.2 1.0 fusion.58
  57.3 1.9 %multiply_add_fusion.5 = f32[2,8,256,128]{3,2,1,0:T(8,128)S(1)} fusion(f32[2,8,256,128]{3,2,1,0:T(8,128)S(1)} %get-tuple-element.498, bf16[256,2,128,1]{0,2,3,1:T(8,128)(2,1)S(1)} %bitcast.85, f32[2,256,256,8]{2,1,3,0:T(8,128)S(1)} %get-tuple-element.472, f32[2,8,256]{2,1,0:T(8,128)S(1)} %max.12, pred[256,256]{0,1:T(8,128)(4,1)S(1)} %compare_and_fusion.3, ...), kind=kOutput, calls=%fused_computation.6.clone.1 | convolution fusion | flops 274726912 | bytes 8617984 | tf_op jit(solution)/shard_map/while/body/eval_jaxpr/ghqk,kgd->ghqd/dot_general | solution.py:71
  60.5 1.3 %copy-done.1 = f32[2,8,256,128]{3,2,1,0:T(8,128)} copy-done((f32[2,8,256,128]{3,2,1,0:T(8,128)}, f32[2,8,256,128]{3,2,1,0:T(8,128)S(1)}, u32[]{:S(2)}) %copy-start.1) | copy-done | bytes 2097176
  61.8 1.9 %copy.33 = f32[2,8,256,128]{2,3,1,0:T(8,128)S(1)} copy(f32[2,8,256,128]{3,2,1,0:T(8,128)} %copy-done.1) | data formatting | bytes 4194304 | tf_op jit(solution)/shard_map/while | solution.py:94
  64.0 16.5 %convolution_convert_fusion = bf16[256,8192]{1,0:T(8,128)(2,1)} fusion(bf16[256,2048]{0,1:T(8,128)(2,1)S(1)} %bitcast.84, bf16[2048,8192]{1,0:T(8,128)(2,1)} %param.12), kind=kOutput, calls=%fused_computation.29 | convolution fusion | flops 8592031744 | bytes 38797312 | tf_op jit(solution)/shard_map/dot_general | solution.py:100
  81.8 18.6 %psum.7 = f32[]{:T(128)} all-reduce(f32[]{:T(128)} %convert_reduce_fusion), channel_id=1, replica_groups=mesh['dp'=2,'context'=4,'tensor'=4] {'dp','context'}, use_global_device_ids=true, to_apply=%region_10.11 | all-reduce | flops 1 | bytes 8 | tf_op jit(solution)/shard_map/psum | solution.py:105
  101.0 22.1 %reduce-scatter.2.cloned.1.call-done = bf16[256,2048]{1,0:T(8,128)(2,1)} async-done(((bf16[256,8192]{1,0:T(8,128)(2,1)}), bf16[256,2048]{1,0:T(8,128)(2,1)}) %reduce-scatter.2.cloned.1.call-update) | async-done | bytes 1048592 | tf_op jit(solution)/shard_map/reduce_scatter | solution.py:101
  123.1 2.4 %fusion.30 = bf16[1,256,2048]{2,1,0:T(8,128)(2,1)} fusion(bf16[256,2048]{1,0:T(8,128)(2,1)} %reduce-scatter.2.cloned.1.call-done, f32[256]{0:T(256)S(1)} %bitcast.89), kind=kLoop, calls=%fused_computation.44 | loop fusion | flops 1572864 | bytes 2098176 | tf_op jit(solution)/shard_map/broadcast_in_dim | solution.py:108
  (55 shorter events, 7.3 us)
Async XLA Ops:
  6.5 4.7 %copy-start.3 = (s32[1,1024]{1,0:T(1,128)S(1)}, s32[1,1024]{1,0:T(1,128)}, u32[]{:S(2)}) copy-start(s32[1,1024]{1,0:T(1,128)} %param.13) | copy-start | bytes 12292
  6.5 116.6 %reduce-scatter.2.cloned.1.call-start = ((), (), s32[]{:S(2)}) async-start(), calls=%async_computation.1 | async-start | bytes 5242880 | tf_op jit(solution)/shard_map/reduce_scatter | solution.py:101
  13.2 1.9 %copy-start = (f32[2,256,256,8]{2,1,3,0:T(8,128)}, f32[2,256,256,8]{2,1,3,0:T(8,128)S(1)}, u32[]{:S(2)}) copy-start(f32[2,256,256,8]{2,1,3,0:T(8,128)S(1)} %get-tuple-element.391) | copy-start | bytes 12582916
  16.9 3.4 %copy-start.2 = (s32[8]{0:T(128)S(1)}, s32[8]{0:T(128)}, u32[]{:S(2)}) copy-start(s32[8]{0:T(128)} %param.15) | copy-start | bytes 100
  20.3 9.7 %collective-permute-start = (bf16[256,256]{0,1:T(8,128)(2,1)}, bf16[256,256]{0,1:T(8,128)(2,1)S(1)}, u32[]{:S(2)}, u32[]{:S(2)}) collective-permute-start(bf16[256,256]{0,1:T(8,128)(2,1)} %get-tuple-element.494), channel_id=1, source_target_pairs={{0,4},{4,8},{8,12},{12,0},{1,5},{5,9},{9,13},{13,1},{2,6},{6,10},{... | collective-permute-start | bytes 393224 | tf_op jit(solution)/shard_map/while/body/eval_jaxpr/ppermute | solution.py:14
  23.4 8.5 %collective-permute-start.1 = (bf16[256,256]{0,1:T(8,128)(2,1)}, bf16[256,256]{0,1:T(8,128)(2,1)S(1)}, u32[]{:S(2)}, u32[]{:S(2)}) collective-permute-start(bf16[256,256]{0,1:T(8,128)(2,1)} %get-tuple-element.495), channel_id=1, source_target_pairs={{0,4},{4,8},{8,12},{12,0},{1,5},{5,9},{9,13},{13,1},{2,6},{6,10},{... | collective-permute-start | bytes 393224 | tf_op jit(solution)/shard_map/while/body/eval_jaxpr/ppermute | solution.py:14
  35.1 8.0 %collective-permute-start = (bf16[256,256]{0,1:T(8,128)(2,1)}, bf16[256,256]{0,1:T(8,128)(2,1)S(1)}, u32[]{:S(2)}, u32[]{:S(2)}) collective-permute-start(bf16[256,256]{0,1:T(8,128)(2,1)} %get-tuple-element.494), channel_id=1, source_target_pairs={{0,4},{4,8},{8,12},{12,0},{1,5},{5,9},{9,13},{13,1},{2,6},{6,10},{... | collective-permute-start | bytes 393224 | tf_op jit(solution)/shard_map/while/body/eval_jaxpr/ppermute | solution.py:14
  35.1 10.0 %collective-permute-start.1 = (bf16[256,256]{0,1:T(8,128)(2,1)}, bf16[256,256]{0,1:T(8,128)(2,1)S(1)}, u32[]{:S(2)}, u32[]{:S(2)}) collective-permute-start(bf16[256,256]{0,1:T(8,128)(2,1)} %get-tuple-element.495), channel_id=1, source_target_pairs={{0,4},{4,8},{8,12},{12,0},{1,5},{5,9},{9,13},{13,1},{2,6},{6,10},{... | collective-permute-start | bytes 393224 | tf_op jit(solution)/shard_map/while/body/eval_jaxpr/ppermute | solution.py:14
  48.3 7.0 %collective-permute-start = (bf16[256,256]{0,1:T(8,128)(2,1)}, bf16[256,256]{0,1:T(8,128)(2,1)S(1)}, u32[]{:S(2)}, u32[]{:S(2)}) collective-permute-start(bf16[256,256]{0,1:T(8,128)(2,1)} %get-tuple-element.494), channel_id=1, source_target_pairs={{0,4},{4,8},{8,12},{12,0},{1,5},{5,9},{9,13},{13,1},{2,6},{6,10},{... | collective-permute-start | bytes 393224 | tf_op jit(solution)/shard_map/while/body/eval_jaxpr/ppermute | solution.py:14
  48.3 8.9 %collective-permute-start.1 = (bf16[256,256]{0,1:T(8,128)(2,1)}, bf16[256,256]{0,1:T(8,128)(2,1)S(1)}, u32[]{:S(2)}, u32[]{:S(2)}) collective-permute-start(bf16[256,256]{0,1:T(8,128)(2,1)} %get-tuple-element.495), channel_id=1, source_target_pairs={{0,4},{4,8},{8,12},{12,0},{1,5},{5,9},{9,13},{13,1},{2,6},{6,10},{... | collective-permute-start | bytes 393224 | tf_op jit(solution)/shard_map/while/body/eval_jaxpr/ppermute | solution.py:14
  60.5 1.4 %copy-start.1 = (f32[2,8,256,128]{3,2,1,0:T(8,128)}, f32[2,8,256,128]{3,2,1,0:T(8,128)S(1)}, u32[]{:S(2)}) copy-start(f32[2,8,256,128]{3,2,1,0:T(8,128)S(1)} %get-tuple-element.334) | copy-start | bytes 6291460
  80.5 0.7 copy-start.4
Sparse Core Ops, SparseCore 0:
  80.7 42.4 reduce-scatter.1
where the time goes:
time: 133 us; the launch traced here: 132 us
  waiting for transfers between devices  39.6 us (30%)
  matrix products  30 us (23%)
  blocking collectives  18.6 us (14%)
  local copies, waits for them, and re-layouts  14.6 us (11%)
  between operations  13.5 us (10%)
  other arithmetic  9.68 us (7%)
  starting transfers between devices  6.25 us (5%)
    reduce_scatter x1, waiting for transfers between devices, per_device(): lax.psum_scatter(partial_value.astype(jnp.bfloat16), 'tensor', scatter_di...  22.1 us
    psum x1, blocking collectives, per_device(): counted = lax.psum(jnp.sum(mask_rows), ('dp', 'context'))  18.6 us
    ppermute x6, waiting for transfers between devices, passed_along(): return lax.ppermute(value, axis, pairs)  17.5 us
    dot_general x1, matrix products, per_device(): jnp.dot(heads_out, out_weight, preferred_element_type=jnp.float32)  16.5 us
    dot_general x4, matrix products, attend(): jnp.einsum('ghqk,kgd->ghqd', probs.astype(jnp.bfloat16), value_heads, pre...  9.06 us
    unnamed x13, local copies, waits for them, and re-layouts  6.9 us
    ppermute x6, starting transfers between devices, passed_along(): return lax.ppermute(value, axis, pairs)  6.25 us
    dot_general x4, matrix products, attend(): jnp.einsum('qghd,kgd->ghqk', query_heads, key_heads, preferred_element_ty...  4.35 us
  transfers between devices with their start and end apart: 7, of which 4 were waited for; matrix products, arithmetic and copies ran while one was open for 6% of the time, Pallas kernels for 0%

commit v1 on v0

v1 whole, which is shorter than its diff:
```python
import functools

import jax
import jax.numpy as jnp
from jax import lax
from jax.experimental import pallas as pl
from jax.experimental.pallas import tpu as pltpu
from jax.sharding import PartitionSpec as P

QH = 64
KVH = 8
HD = 128
LEAD = 2
HEADS_STEP = 2


def kernel(
    sizes,
    q_hbm,
    k_hbm,
    v_hbm,
    w_hbm,
    seg_ref,
    mask_ref,
    order_ref,
    out_hbm,
    q_buf,
    kv_buf,
    w_buf,
    best_buf,
    acc_buf,
    heads_buf,
    bias_buf,
    masks_buf,
    sib_send,
    sib_recv,
    far_send,
    far_recv,
    own_buf,
    out_buf,
    q_sem,
    kv_load_sem,
    w_sem,
    kv_send_sem,
    kv_recv_sem,
    mask_send_sem,
    mask_recv_sem,
    mask_load_sem,
    sib_send_sem,
    sib_recv_sem,
    far_send_sem,
    far_recv_sem,
    out_sem,
):
    n_dp, n_ctx, n_t = sizes
    rows = q_hbm.shape[1]
    span_rows = rows // 2
    heads_dev = q_hbm.shape[2] // HD
    group = QH // KVH
    kv_dev = kv_buf.shape[1]
    per_kv = heads_dev // kv_dev
    chunk = w_buf.shape[2]
    n_far = n_t // 2
    features = w_hbm.shape[1] // n_t
    per_block = features // chunk
    total = n_far * per_block
    n_masks = n_dp * n_ctx
    factor = HD ** (-0.5)

    dp = lax.axis_index("dp")
    z = lax.axis_index("context")
    t = lax.axis_index("tensor")
    core = lax.rem(t, 2)
    y = lax.div(t, 2)
    sibling = t + 1 - 2 * core
    me = dp * n_ctx + z

    def mask_peer(k):
        index = lax.rem(me + k, n_masks)
        return {"dp": lax.div(index, n_ctx), "context": lax.rem(index, n_ctx), "tensor": t}

    def at(ctx, tensor):
        return {"dp": dp, "context": ctx, "tensor": tensor}

    def far_peer(dy):
        return lax.rem(y + dy, n_far) * 2 + core

    kv_col = lax.div(t * heads_dev, group) * HD

    def kv_loads():
        for g in range(kv_dev):
            for which, src in ((0, k_hbm), (1, v_hbm)):
                col = pl.multiple_of(kv_col + g * HD, HD)
                yield pltpu.make_async_copy(
                    src.at[0, :, pl.ds(col, HD)],
                    kv_buf.at[z, g, which],
                    kv_load_sem.at[g, which],
                )

    for copy in kv_loads():
        copy.start()
    q_copy = pltpu.make_async_copy(q_hbm.at[0], q_buf, q_sem)
    q_copy.start()
    mask_copy = pltpu.make_async_copy(mask_ref, masks_buf.at[me], mask_load_sem)
    mask_copy.start()

    barrier = pltpu.get_barrier_semaphore()
    for k in range(1, n_masks):
        pl.semaphore_signal(barrier, inc=1, device_id=mask_peer(k))
    pl.semaphore_signal(barrier, inc=1, device_id=at(z, sibling))
    for dy in range(1, n_far):
        pl.semaphore_signal(barrier, inc=1, device_id=at(z, far_peer(dy)))

    def block_of(i):
        dy = lax.rem(lax.div(i, per_block) + 1, n_far)
        return dy, lax.rem(i, per_block), lax.rem(y + dy, n_far)

    def w_chunk(i, other):
        _, j, far_y = block_of(i)
        c = 1 - core if other else core
        return (far_y * 2 + c) * per_block + j

    def w_load(index):
        col = pl.multiple_of(index * chunk, chunk)
        return pltpu.make_async_copy(
            w_hbm.at[:, pl.ds(col, chunk)], w_buf.at[index], w_sem.at[index]
        )

    @pl.loop(0, total)
    def _(i):
        w_load(w_chunk(i, True)).start()
        w_load(w_chunk(i, False)).start()

    def kv_send(owner, g, direction):
        return pltpu.make_async_remote_copy(
            src_ref=kv_buf.at[owner, g],
            dst_ref=kv_buf.at[owner, g],
            send_sem=kv_send_sem.at[(direction + 1) // 2, owner, g],
            recv_sem=kv_recv_sem.at[owner, g],
            device_id=at(z + direction, t),
        )

    for copy in kv_loads():
        copy.wait()
    pl.semaphore_wait(barrier, n_masks + n_far - 1)

    for g in range(kv_dev):
        for direction in (1, -1):

            @pl.when((z + direction >= 0) & (z + direction < n_ctx))
            def _():
                kv_send(z, g, direction).start()

    mask_copy.wait()

    def mask_send(k):
        return pltpu.make_async_remote_copy(
            src_ref=masks_buf.at[me],
            dst_ref=masks_buf.at[me],
            send_sem=mask_send_sem.at[k],
            recv_sem=mask_recv_sem.at[k],
            device_id=mask_peer(k),
        )

    for k in range(1, n_masks):
        mask_send(k).start()

    lane = lax.broadcasted_iota(jnp.int32, (1, rows), 1)

    def pos_row(owner):
        first = order_ref[2 * owner]
        second = order_ref[2 * owner + 1]
        return (
            jnp.where(lane < span_rows, first, second) * span_rows
            + jnp.where(lane < span_rows, lane, lane - span_rows)
        ).astype(jnp.float32)

    def seg_row(owner):
        return seg_ref[:, pl.ds(pl.multiple_of(owner * rows, rows), rows)].astype(jnp.float32)

    diagonal = lax.broadcasted_iota(jnp.int32, (rows, rows), 0) == lax.broadcasted_iota(
        jnp.int32, (rows, rows), 1
    )

    def as_column(row):
        return jnp.sum(jnp.where(diagonal, row, 0.0), axis=1, keepdims=True)

    query_pos = as_column(pos_row(z))
    query_seg = as_column(seg_row(z))
    q_copy.wait()

    def attend(owner, first):
        allowed = (query_seg == seg_row(owner)) & (query_pos >= pos_row(owner))
        bias_buf[...] = jnp.where(allowed, 0.0, -1e30)
        ones = jnp.ones((rows, HD), jnp.bfloat16)
        for g in range(kv_dev):
            keys = kv_buf[owner, g, 0]
            wide = jnp.concatenate([kv_buf[owner, g, 1], ones], axis=1)

            @pl.loop(0, per_kv // HEADS_STEP)
            def _(step):
                for u in range(HEADS_STEP):
                    head = g * per_kv + step * HEADS_STEP + u
                    query = q_buf[:, pl.ds(pl.multiple_of(head * HD, HD), HD)]
                    scores = lax.dot_general(
                        query, keys, (((1,), (1,)), ((), ())), preferred_element_type=jnp.float32
                    )
                    scores = scores * factor + bias_buf[...]
                    top = jnp.max(scores, axis=1, keepdims=True)
                    if first:
                        best = top
                    else:
                        old = best_buf[head][:, :1]
                        best = jnp.maximum(old, top)
                        correct = jnp.exp(old - best)
                    probs = jnp.exp(scores - best).astype(jnp.bfloat16)
                    update = jnp.dot(probs, wide, preferred_element_type=jnp.float32)
                    if not first:
                        update = update + acc_buf[head] * correct
                    acc_buf[head] = update
                    best_buf[head] = jnp.broadcast_to(best, (rows, HD))

    attend(z, True)

    @pl.loop(1, n_ctx)
    def _(s):
        for g in range(kv_dev):
            for direction in (1, -1):
                owner = z - direction * s

                @pl.when((owner >= 0) & (owner < n_ctx))
                def _():
                    kv_send(owner, g, direction).wait_recv()

                    @pl.when((z + direction >= 0) & (z + direction < n_ctx))
                    def _():
                        kv_send(owner, g, direction).start()

        @pl.loop(0, 2)
        def _(side):
            owner = z - (1 - 2 * side) * s

            @pl.when((owner >= 0) & (owner < n_ctx))
            def _():
                attend(owner, False)

    for head in range(heads_dev):
        state = acc_buf[head]
        heads_buf[:, head * HD : (head + 1) * HD] = (state[:, :HD] / state[:, HD:]).astype(
            jnp.bfloat16
        )

    def sib_copy(i):
        return pltpu.make_async_remote_copy(
            src_ref=sib_send.at[i],
            dst_ref=sib_recv.at[i],
            send_sem=sib_send_sem.at[i],
            recv_sem=sib_recv_sem.at[i],
            device_id=at(z, sibling),
        )

    def far_copy(i):
        dy, _, _ = block_of(i)
        return pltpu.make_async_remote_copy(
            src_ref=far_send.at[i],
            dst_ref=far_recv.at[i],
            send_sem=far_send_sem.at[i],
            recv_sem=far_recv_sem.at[i],
            device_id=at(z, far_peer(dy)),
        )

    n_sent = total - per_block

    @pl.loop(0, total + LEAD)
    def _(step):
        @pl.when(step < total)
        def _():
            index = w_chunk(step, True)
            w_load(index).wait()
            sib_send[step] = jnp.dot(
                heads_buf[...], w_buf[index], preferred_element_type=jnp.float32
            ).astype(jnp.bfloat16)
            sib_copy(step).start()

        @pl.when(step >= LEAD)
        def _():
            i = step - LEAD
            index = w_chunk(i, False)
            w_load(index).wait()
            value = jnp.dot(heads_buf[...], w_buf[index], preferred_element_type=jnp.float32)
            sib_copy(i).wait_recv()
            value = value + sib_recv[i].astype(jnp.float32)

            @pl.when(i < n_sent)
            def _():
                far_send[i] = value.astype(jnp.bfloat16)
                far_copy(i).start()

            @pl.when(i >= n_sent)
            def _():
                own_buf[i - n_sent] = value

    for k in range(1, n_masks):
        mask_send(k).wait_recv()
    marks = jnp.sum(masks_buf[...].astype(jnp.float32), axis=0)
    count = jnp.sum(marks, axis=1, keepdims=True)
    mine = masks_buf[me].astype(jnp.float32)
    scale_all = float(n_dp * n_ctx * rows)
    weight = as_column(mine * scale_all / count)

    def out_copy(j):
        return pltpu.make_async_copy(
            out_buf.at[j],
            out_hbm.at[0, :, pl.ds(pl.multiple_of(j * chunk, chunk), chunk)],
            out_sem.at[j],
        )

    @pl.loop(0, per_block)
    def _(j):
        value = own_buf[j]
        for dy in range(1, n_far):
            i = (dy - 1) * per_block + j
            far_copy(i).wait_recv()
            value = value + far_recv[i].astype(jnp.float32)
        out_buf[j] = (value * weight).astype(jnp.bfloat16)
        out_copy(j).start()

    for k in range(1, n_masks):
        mask_send(k).wait_send()
    for direction in (1, -1):

        @pl.when((z + direction >= 0) & (z + direction < n_ctx))
        def _():
            @pl.loop(0, n_ctx)
            def _(s):
                owner = z - direction * s

                @pl.when((owner >= 0) & (owner < n_ctx))
                def _():
                    for g in range(kv_dev):
                        kv_send(owner, g, direction).wait_send()

    @pl.loop(0, total)
    def _(i):
        sib_copy(i).wait_send()

    @pl.loop(0, n_sent)
    def _(i):
        far_copy(i).wait_send()

    @pl.loop(0, per_block)
    def _(j):
        out_copy(j).wait()


def per_device(sizes, queries, keys, values, out_weight, segment_ids, loss_mask, span_order):
    n_dp, n_ctx, n_t = sizes
    rows = queries.shape[1]
    heads_dev = queries.shape[2] // HD
    kv_dev = max(1, heads_dev // (QH // KVH))
    depth, width = out_weight.shape
    features = width // n_t
    chunk = min(256, features)
    per_block = features // chunk
    n_far = n_t // 2
    total = n_far * per_block
    n_sent = max(1, total - per_block)
    n_masks = n_dp * n_ctx
    bf16, f32 = jnp.bfloat16, jnp.float32
    dma = pltpu.SemaphoreType.DMA
    anywhere = pl.BlockSpec(memory_space=pl.ANY)
    vmem = pl.BlockSpec(memory_space=pltpu.VMEM)
    return pl.pallas_call(
        functools.partial(kernel, sizes),
        out_shape=jax.ShapeDtypeStruct((1, rows, features), bf16),
        in_specs=[
            anywhere,
            anywhere,
            anywhere,
            anywhere,
            vmem,
            anywhere,
            pl.BlockSpec(memory_space=pltpu.SMEM),
        ],
        out_specs=anywhere,
        scratch_shapes=[
            pltpu.VMEM((rows, heads_dev * HD), bf16),
            pltpu.VMEM((n_ctx, kv_dev, 2, rows, HD), bf16),
            pltpu.VMEM((width // chunk, depth, chunk), bf16),
            pltpu.VMEM((heads_dev, rows, HD), f32),
            pltpu.VMEM((heads_dev, rows, 2 * HD), f32),
            pltpu.VMEM((rows, heads_dev * HD), bf16),
            pltpu.VMEM((rows, rows), f32),
            pltpu.VMEM((n_masks, 1, rows), jnp.int32),
            pltpu.VMEM((total, rows, chunk), bf16),
            pltpu.VMEM((total, rows, chunk), bf16),
            pltpu.VMEM((n_sent, rows, chunk), bf16),
            pltpu.VMEM((n_sent, rows, chunk), bf16),
            pltpu.VMEM((per_block, rows, chunk), f32),
            pltpu.VMEM((per_block, rows, chunk), bf16),
            dma,
            dma((kv_dev, 2)),
            dma((width // chunk,)),
            dma((2, n_ctx, kv_dev)),
            dma((n_ctx, kv_dev)),
            dma((n_masks,)),
            dma((n_masks,)),
            dma,
            dma((total,)),
            dma((total,)),
            dma((n_sent,)),
            dma((n_sent,)),
            dma((per_block,)),
        ],
        compiler_params=pltpu.CompilerParams(
            collective_id=0, has_side_effects=True, vmem_limit_bytes=62 * 1024 * 1024
        ),
    )(queries, keys, values, out_weight, segment_ids, loss_mask, span_order)


def solution(mesh):
    sizes = (mesh.shape["dp"], mesh.shape["context"], mesh.shape["tensor"])
    in_specs = (
        P("dp", "context", "tensor"),
        P("dp", "context", None),
        P("dp", "context", None),
        P("tensor", None),
        P("dp", None),
        P("dp", "context"),
        P(),
    )
    out_specs = P("dp", "context", "tensor")
    return jax.shard_map(
        functools.partial(per_device, sizes),
        mesh=mesh,
        in_specs=in_specs,
        out_specs=out_specs,
        check_vma=False,
    )
```

time: 133 us -> 73 us (0.55)
  Pallas kernels: 0 us -> 70.5 us
  waiting for transfers between devices: 39.6 us -> 0 us
  matrix products: 30 us -> 0 us
  blocking collectives: 18.6 us -> 0 us
  between operations: 13.5 us -> 0.01 us
  local copies, waits for them, and re-layouts: 14.6 us -> 2.3 us
  other arithmetic: 9.68 us -> 0 us
  starting transfers between devices: 6.25 us -> 0 us
    pallas_call x0 -> x1, Pallas kernels: none -> 70.5 us  [per_device(): pl.pallas_call(functools.partial(kernel, sizes), out_shape=jax.ShapeDtype...]
    dot_general x9 -> x0, matrix products: 30 us -> none  [the longest x1 16.5 us: per_device(): jnp.dot(heads_out, out_weight, preferred_element_type=jnp.float32)]
    reduce_scatter x1 -> x0, waiting for transfers between devices: 22.1 us -> none  [per_device(): lax.psum_scatter(partial_value.astype(jnp.bfloat16), 'tensor', scatter_di...]
    psum x1 -> x0, blocking collectives: 18.6 us -> none  [per_device(): counted = lax.psum(jnp.sum(mask_rows), ('dp', 'context'))]
    ppermute x6 -> x0, waiting for transfers between devices: 17.5 us -> none  [passed_along(): return lax.ppermute(value, axis, pairs)]
    while x11 -> x0, local copies, waits for them, and re-layouts: 6.49 us -> none
    ppermute x6 -> x0, starting transfers between devices: 6.25 us -> none  [passed_along(): return lax.ppermute(value, axis, pairs)]
    reduce_sum x9 -> x0, other arithmetic: 5.67 us -> none  [the longest x4 4.08 us: attend(): total = total * correct + jnp.sum(probs, axis=-1)]
  transfers between devices with their start and end apart: 7 -> 0, of which waited for: 4 -> 0; matrix products, arithmetic and copies ran while one was open for 6% -> 0% of each run, Pallas kernels for 0% -> 0%
where the time goes in v1:
time: 73 us; the launch traced here: 72.8 us
  Pallas kernels  70.5 us (97%)
  local copies, waits for them, and re-layouts  2.3 us (3%)
    pallas_call x1, Pallas kernels, per_device(): pl.pallas_call(functools.partial(kernel, sizes), out_shape=jax.ShapeDtype...  70.5 us
    unnamed x1, local copies, waits for them, and re-layouts  2.3 us

profile of v1, /device:TPU:0, one launch (start us, length us, event | category | flops | bytes accessed | tf_op | source)
XLA Modules:
  0.0 72.8 jit_solution(8775785203896941074)
XLA Ops:
  0.0 70.5 %shard_map.73 = bf16[1,256,2048]{2,1,0:T(8,128)(2,1)} custom-call(bf16[1,256,2048]{2,1,0:T(8,128)(2,1)} %q_hbm.1, bf16[1,256,1024]{2,1,0:T(8,128)(2,1)} %k_hbm.1, bf16[1,256,1024]{2,1,0:T(8,128)(2,1)} %v_hbm.1, bf16[2048,8192]{1,0:T(8,128)(2,1)} %w_hbm.1, s32[1,1024]{1,0:T(1,128)} %seg_ref.1, s32[1,256]{1,0:T(1,128)} %mask_ref.1, s32[8]{0:T(128)} %order_ref.1), custom_call_target="tpu_custom_call" | custom-call | tf_op jit(solution)/shard_map/pallas_call | solution.py:373
  70.5 2.3 %copy.9 = bf16[1,256,2048]{2,1,0:T(8,128)(2,1)} copy(bf16[1,256,2048]{2,1,0:T(8,128)(2,1)} %shard_map.73) | data formatting | bytes 2097152

commit v2 on v1

--- a/solution.py
+++ b/solution.py
@@ -1,4 +1,5 @@
 import functools
+import math
 
 import jax
 import jax.numpy as jnp
@@ -11,7 +12,8 @@
 KVH = 8
 HD = 128
 LEAD = 2
-HEADS_STEP = 2
+HEADS_STEP = 4
+ONES = 16
 
 
 def kernel(
@@ -23,8 +25,10 @@
     seg_ref,
     mask_ref,
     order_ref,
-    out_hbm,
+    out_ref,
     q_buf,
+    qt_buf,
+    vt_buf,
     kv_buf,
     w_buf,
     best_buf,
@@ -37,7 +41,6 @@
     far_send,
     far_recv,
     own_buf,
-    out_buf,
     q_sem,
     kv_load_sem,
     w_sem,
@@ -50,7 +53,6 @@
     sib_recv_sem,
     far_send_sem,
     far_recv_sem,
-    out_sem,
 ):
     n_dp, n_ctx, n_t = sizes
     rows = q_hbm.shape[1]
@@ -65,7 +67,7 @@
     per_block = features // chunk
     total = n_far * per_block
     n_masks = n_dp * n_ctx
-    factor = HD ** (-0.5)
+    factor = HD ** (-0.5) * math.log2(math.e)
 
     dp = lax.axis_index("dp")
     z = lax.axis_index("context")
@@ -185,40 +187,44 @@
     def as_column(row):
         return jnp.sum(jnp.where(diagonal, row, 0.0), axis=1, keepdims=True)
 
-    query_pos = as_column(pos_row(z))
-    query_seg = as_column(seg_row(z))
+    query_pos = pos_row(z)
+    query_seg = seg_row(z)
     q_copy.wait()
 
+    @pl.loop(0, heads_dev)
+    def _(head):
+        part = q_buf[:, pl.ds(pl.multiple_of(head * HD, HD), HD)]
+        qt_buf[head] = jnp.transpose(part, (1, 0))
+
     def attend(owner, first):
-        allowed = (query_seg == seg_row(owner)) & (query_pos >= pos_row(owner))
+        key_seg = as_column(seg_row(owner))
+        key_pos = as_column(pos_row(owner))
+        allowed = (key_seg == query_seg) & (query_pos >= key_pos)
         bias_buf[...] = jnp.where(allowed, 0.0, -1e30)
-        ones = jnp.ones((rows, HD), jnp.bfloat16)
         for g in range(kv_dev):
-            keys = kv_buf[owner, g, 0]
-            wide = jnp.concatenate([kv_buf[owner, g, 1], ones], axis=1)
-
-            @pl.loop(0, per_kv // HEADS_STEP)
-            def _(step):
-                for u in range(HEADS_STEP):
-                    head = g * per_kv + step * HEADS_STEP + u
-                    query = q_buf[:, pl.ds(pl.multiple_of(head * HD, HD), HD)]
-                    scores = lax.dot_general(
-                        query, keys, (((1,), (1,)), ((), ())), preferred_element_type=jnp.float32
-                    )
-                    scores = scores * factor + bias_buf[...]
-                    top = jnp.max(scores, axis=1, keepdims=True)
-                    if first:
-                        best = top
-                    else:
-                        old = best_buf[head][:, :1]
-                        best = jnp.maximum(old, top)
-                        correct = jnp.exp(old - best)
-                    probs = jnp.exp(scores - best).astype(jnp.bfloat16)
-                    update = jnp.dot(probs, wide, preferred_element_type=jnp.float32)
-                    if not first:
-                        update = update + acc_buf[head] * correct
-                    acc_buf[head] = update
-                    best_buf[head] = jnp.broadcast_to(best, (rows, HD))
+            vt_buf[g, :HD] = jnp.transpose(kv_buf[owner, g, 1], (1, 0))
+            vt_buf[g, HD:] = jnp.ones((ONES, rows), jnp.bfloat16)
+
+        @pl.loop(0, heads_dev // HEADS_STEP)
+        def _(step):
+            for u in range(HEADS_STEP):
+                head = step * HEADS_STEP + u
+                g = lax.div(head, per_kv)
+                scores = jnp.dot(
+                    kv_buf[owner, g, 0], qt_buf[head], preferred_element_type=jnp.float32
+                )
+                scores = scores + bias_buf[...]
+                best = jnp.max(scores, axis=0, keepdims=True)
+                if not first:
+                    old = best_buf[head]
+                    best = jnp.maximum(old, best)
+                    correct = jnp.exp2((old - best) * factor)
+                probs = jnp.exp2((scores - best) * factor).astype(jnp.bfloat16)
+                update = jnp.dot(vt_buf[g], probs, preferred_element_type=jnp.float32)
+                if not first:
+                    update = update + acc_buf[head] * correct
+                acc_buf[head] = update
+                best_buf[head] = best
 
     attend(z, True)
 
@@ -245,9 +251,9 @@
                 attend(owner, False)
 
     for head in range(heads_dev):
-        state = acc_buf[head]
-        heads_buf[:, head * HD : (head + 1) * HD] = (state[:, :HD] / state[:, HD:]).astype(
-            jnp.bfloat16
+        mixed = acc_buf[head, :HD] / acc_buf[head, HD : HD + 1]
+        heads_buf[:, head * HD : (head + 1) * HD] = jnp.transpose(
+            mixed.astype(jnp.bfloat16), (1, 0)
         )
 
     def sib_copy(i):
@@ -308,13 +314,6 @@
     scale_all = float(n_dp * n_ctx * rows)
     weight = as_column(mine * scale_all / count)
 
-    def out_copy(j):
-        return pltpu.make_async_copy(
-            out_buf.at[j],
-            out_hbm.at[0, :, pl.ds(pl.multiple_of(j * chunk, chunk), chunk)],
-            out_sem.at[j],
-        )
-
     @pl.loop(0, per_block)
     def _(j):
         value = own_buf[j]
@@ -322,8 +321,8 @@
             i = (dy - 1) * per_block + j
             far_copy(i).wait_recv()
             value = value + far_recv[i].astype(jnp.float32)
-        out_buf[j] = (value * weight).astype(jnp.bfloat16)
-        out_copy(j).start()
+        col = pl.multiple_of(j * chunk, chunk)
+        out_ref[0, :, pl.ds(col, chunk)] = (value * weight).astype(jnp.bfloat16)
 
     for k in range(1, n_masks):
         mask_send(k).wait_send()
@@ -347,10 +346,6 @@
     @pl.loop(0, n_sent)
     def _(i):
         far_copy(i).wait_send()
-
-    @pl.loop(0, per_block)
-    def _(j):
-        out_copy(j).wait()
 
 
 def per_device(sizes, queries, keys, values, out_weight, segment_ids, loss_mask, span_order):
@@ -372,7 +367,7 @@
     vmem = pl.BlockSpec(memory_space=pltpu.VMEM)
     return pl.pallas_call(
         functools.partial(kernel, sizes),
-        out_shape=jax.ShapeDtypeStruct((1, rows, features), bf16),
+        out_shape=pltpu.VMEM((1, rows, features), bf16),
         in_specs=[
             anywhere,
             anywhere,
@@ -382,13 +377,15 @@
             anywhere,
             pl.BlockSpec(memory_space=pltpu.SMEM),
         ],
-        out_specs=anywhere,
+        out_specs=vmem,
         scratch_shapes=[
             pltpu.VMEM((rows, heads_dev * HD), bf16),
+            pltpu.VMEM((heads_dev, HD, rows), bf16),
+            pltpu.VMEM((kv_dev, HD + ONES, rows), bf16),
             pltpu.VMEM((n_ctx, kv_dev, 2, rows, HD), bf16),
             pltpu.VMEM((width // chunk, depth, chunk), bf16),
-            pltpu.VMEM((heads_dev, rows, HD), f32),
-            pltpu.VMEM((heads_dev, rows, 2 * HD), f32),
+            pltpu.VMEM((heads_dev, 1, rows), f32),
+            pltpu.VMEM((heads_dev, HD + ONES, rows), f32),
             pltpu.VMEM((rows, heads_dev * HD), bf16),
             pltpu.VMEM((rows, rows), f32),
             pltpu.VMEM((n_masks, 1, rows), jnp.int32),
@@ -397,7 +394,6 @@
             pltpu.VMEM((n_sent, rows, chunk), bf16),
             pltpu.VMEM((n_sent, rows, chunk), bf16),
             pltpu.VMEM((per_block, rows, chunk), f32),
-            pltpu.VMEM((per_block, rows, chunk), bf16),
             dma,
             dma((kv_dev, 2)),
             dma((width // chunk,)),
@@ -410,10 +406,9 @@
             dma((total,)),
             dma((n_sent,)),
             dma((n_sent,)),
-            dma((per_block,)),
         ],
         compiler_params=pltpu.CompilerParams(
-            collective_id=0, has_side_effects=True, vmem_limit_bytes=62 * 1024 * 1024
+            collective_id=0, has_side_effects=True, vmem_limit_bytes=60 * 1024 * 1024
         ),
     )(queries, keys, values, out_weight, segment_ids, loss_mask, span_order)
 

time: 73 us -> 65.9 us (0.903)
  Pallas kernels: 70.5 us -> 64.7 us
  local copies, waits for them, and re-layouts: 2.3 us -> 0.97 us
    pallas_call x1, Pallas kernels: 70.5 us -> 64.7 us  [per_device(): pl.pallas_call(functools.partial(kernel, sizes), out_shape=pltpu.VMEM((1,...]
    unnamed x1, local copies, waits for them, and re-layouts: 2.3 us -> 0.97 us
where the time goes in v2:
time: 65.9 us; the launch traced here: 65.7 us
  Pallas kernels  64.7 us (98%)
  local copies, waits for them, and re-layouts  0.97 us (1%)
    pallas_call x1, Pallas kernels, per_device(): pl.pallas_call(functools.partial(kernel, sizes), out_shape=pltpu.VMEM((1,...  64.7 us

profile of v2, /device:TPU:0, one launch (start us, length us, event | category | flops | bytes accessed | tf_op | source)
XLA Modules:
  0.0 65.7 jit_solution(5883910782264957795)
XLA Ops:
  0.0 64.7 %shard_map.73 = bf16[1,256,2048]{2,1,0:T(8,128)(2,1)S(1)} custom-call(bf16[1,256,2048]{2,1,0:T(8,128)(2,1)} %q_hbm.1, bf16[1,256,1024]{2,1,0:T(8,128)(2,1)} %k_hbm.1, bf16[1,256,1024]{2,1,0:T(8,128)(2,1)} %v_hbm.1, bf16[2048,8192]{1,0:T(8,128)(2,1)} %w_hbm.1, s32[1,1024]{1,0:T(1,128)} %seg_ref.1, s32[1,256]{1,0:T(1,128)} %mask_ref.1, s32[8]{0:T(128)} %order_ref.1), custom_call_target="tpu_custom_call" | custom-call | tf_op jit(solution)/shard_map/pallas_call | solution.py:368
  64.7 1.0 %copy.9 = bf16[1,256,2048]{2,1,0:T(8,128)(2,1)} copy(bf16[1,256,2048]{2,1,0:T(8,128)(2,1)S(1)} %shard_map.73) | data formatting | bytes 2097152

commit v3 on v2

--- a/solution.py
+++ b/solution.py
@@ -12,7 +12,7 @@
 KVH = 8
 HD = 128
 LEAD = 2
-HEADS_STEP = 4
+HEADS_STEP = 8
 ONES = 16
 
 
@@ -61,6 +61,7 @@
     group = QH // KVH
     kv_dev = kv_buf.shape[1]
     per_kv = heads_dev // kv_dev
+    together = min(HEADS_STEP, heads_dev)
     chunk = w_buf.shape[2]
     n_far = n_t // 2
     features = w_hbm.shape[1] // n_t
@@ -205,26 +206,37 @@
             vt_buf[g, :HD] = jnp.transpose(kv_buf[owner, g, 1], (1, 0))
             vt_buf[g, HD:] = jnp.ones((ONES, rows), jnp.bfloat16)
 
-        @pl.loop(0, heads_dev // HEADS_STEP)
+        @pl.loop(0, heads_dev // together)
         def _(step):
-            for u in range(HEADS_STEP):
-                head = step * HEADS_STEP + u
-                g = lax.div(head, per_kv)
-                scores = jnp.dot(
-                    kv_buf[owner, g, 0], qt_buf[head], preferred_element_type=jnp.float32
-                )
-                scores = scores + bias_buf[...]
-                best = jnp.max(scores, axis=0, keepdims=True)
-                if not first:
-                    old = best_buf[head]
-                    best = jnp.maximum(old, best)
-                    correct = jnp.exp2((old - best) * factor)
-                probs = jnp.exp2((scores - best) * factor).astype(jnp.bfloat16)
-                update = jnp.dot(vt_buf[g], probs, preferred_element_type=jnp.float32)
-                if not first:
-                    update = update + acc_buf[head] * correct
-                acc_buf[head] = update
-                best_buf[head] = best
+            heads = [step * together + u for u in range(together)]
+            kv_heads = [lax.div(head, per_kv) for head in heads]
+            bias = bias_buf[...]
+            scores = [
+                jnp.dot(kv_buf[owner, g, 0], qt_buf[head], preferred_element_type=jnp.float32)
+                + bias
+                for head, g in zip(heads, kv_heads)
+            ]
+            best = [jnp.max(each, axis=0, keepdims=True) for each in scores]
+            if not first:
+                old = [best_buf[head] for head in heads]
+                best = [jnp.maximum(was, now) for was, now in zip(old, best)]
+                correct = [jnp.exp2((was - now) * factor) for was, now in zip(old, best)]
+            probs = [
+                jnp.exp2((each - top) * factor).astype(jnp.bfloat16)
+                for each, top in zip(scores, best)
+            ]
+            update = [
+                jnp.dot(vt_buf[g], each, preferred_element_type=jnp.float32)
+                for g, each in zip(kv_heads, probs)
+            ]
+            if not first:
+                update = [
+                    each + acc_buf[head] * scale
+                    for head, each, scale in zip(heads, update, correct)
+                ]
+            for head, each, top in zip(heads, update, best):
+                acc_buf[head] = each
+                best_buf[head] = top
 
     attend(z, True)
 

time: 65.9 us -> 57 us (0.86)
  Pallas kernels: 64.7 us -> 55.8 us
    pallas_call x1, Pallas kernels: 64.7 us -> 55.8 us  [per_device(): pl.pallas_call(functools.partial(kernel, sizes), out_shape=pltpu.VMEM((1,...]
where the time goes in v3:
time: 57 us; the launch traced here: 56.8 us
  Pallas kernels  55.8 us (98%)
  local copies, waits for them, and re-layouts  0.97 us (2%)
    pallas_call x1, Pallas kernels, per_device(): pl.pallas_call(functools.partial(kernel, sizes), out_shape=pltpu.VMEM((1,...  55.8 us

profile of v3, /device:TPU:0, one launch (start us, length us, event | category | flops | bytes accessed | tf_op | source)
XLA Modules:
  0.0 56.8 jit_solution(12084883265704984736)
XLA Ops:
  0.0 55.8 %shard_map.73 = bf16[1,256,2048]{2,1,0:T(8,128)(2,1)S(1)} custom-call(bf16[1,256,2048]{2,1,0:T(8,128)(2,1)} %q_hbm.1, bf16[1,256,1024]{2,1,0:T(8,128)(2,1)} %k_hbm.1, bf16[1,256,1024]{2,1,0:T(8,128)(2,1)} %v_hbm.1, bf16[2048,8192]{1,0:T(8,128)(2,1)} %w_hbm.1, s32[1,1024]{1,0:T(1,128)} %seg_ref.1, s32[1,256]{1,0:T(1,128)} %mask_ref.1, s32[8]{0:T(128)} %order_ref.1), custom_call_target="tpu_custom_call" | custom-call | tf_op jit(solution)/shard_map/pallas_call | solution.py:380
  55.8 1.0 %copy.9 = bf16[1,256,2048]{2,1,0:T(8,128)(2,1)} copy(bf16[1,256,2048]{2,1,0:T(8,128)(2,1)S(1)} %shard_map.73) | data formatting | bytes 2097152

commit v4 on v3

--- a/solution.py
+++ b/solution.py
@@ -12,7 +12,7 @@
 KVH = 8
 HD = 128
 LEAD = 2
-HEADS_STEP = 8
+HEADS_STEP = 16
 ONES = 16
 
 
@@ -240,8 +240,7 @@
 
     attend(z, True)
 
-    @pl.loop(1, n_ctx)
-    def _(s):
+    def relay(s):
         for g in range(kv_dev):
             for direction in (1, -1):
                 owner = z - direction * s
@@ -254,13 +253,24 @@
                     def _():
                         kv_send(owner, g, direction).start()
 
+    relay(1)
+
+    @pl.loop(1, n_ctx)
+    def _(s):
+        has_left = 1 - lax.div(s - z + n_ctx - 1, n_ctx)
+
         @pl.loop(0, 2)
-        def _(side):
+        def _(k):
+            side = k * has_left + (1 - k) * (1 - has_left)
             owner = z - (1 - 2 * side) * s
 
             @pl.when((owner >= 0) & (owner < n_ctx))
             def _():
                 attend(owner, False)
+
+            @pl.when((k == 0) & (s + 1 < n_ctx))
+            def _():
+                relay(s + 1)
 
     for head in range(heads_dev):
         mixed = acc_buf[head, :HD] / acc_buf[head, HD : HD + 1]

time: 57 us -> 56.5 us (level)
  no operation moved by 1% of the time
where the time goes in v4:
time: 56.5 us; the launch traced here: 56.4 us
  Pallas kernels  55.4 us (98%)
  local copies, waits for them, and re-layouts  0.97 us (2%)
    pallas_call x1, Pallas kernels, per_device(): pl.pallas_call(functools.partial(kernel, sizes), out_shape=pltpu.VMEM((1,...  55.4 us

profile of v4, /device:TPU:0, one launch (start us, length us, event | category | flops | bytes accessed | tf_op | source)
XLA Modules:
  0.0 56.4 jit_solution(15774856417565582362)
XLA Ops:
  0.0 55.4 %shard_map.73 = bf16[1,256,2048]{2,1,0:T(8,128)(2,1)S(1)} custom-call(bf16[1,256,2048]{2,1,0:T(8,128)(2,1)} %q_hbm.1, bf16[1,256,1024]{2,1,0:T(8,128)(2,1)} %k_hbm.1, bf16[1,256,1024]{2,1,0:T(8,128)(2,1)} %v_hbm.1, bf16[2048,8192]{1,0:T(8,128)(2,1)} %w_hbm.1, s32[1,1024]{1,0:T(1,128)} %seg_ref.1, s32[1,256]{1,0:T(1,128)} %mask_ref.1, s32[8]{0:T(128)} %order_ref.1), custom_call_target="tpu_custom_call" | custom-call | tf_op jit(solution)/shard_map/pallas_call | solution.py:390
  55.4 1.0 %copy.9 = bf16[1,256,2048]{2,1,0:T(8,128)(2,1)} copy(bf16[1,256,2048]{2,1,0:T(8,128)(2,1)S(1)} %shard_map.73) | data formatting | bytes 2097152
